TPU v7x, 32 devices: a whole 2x2x4 slice. The times are simulated.
32 devices in a mesh: pts: 8 (over y, x, core), wid: 4 (over z).
Axes of the slice: x: 2, y: 2, z: 4, core: 2. Of those that a mesh axis runs over, the one named last changes fastest.
Arguments:
- vertex_features: bfloat16 [90112, 512], P('pts'), may hold values from -40 to 40, as said below
- entry_matrix: bfloat16 [512, 512], P(None, 'wid'), may hold values from -2 to 2, as said below
- partition_matrix: bfloat16 [64, 32], replicated, may hold values from -3 to 3, as said below
- sharpness_matrix: float32 [64], replicated, may hold values from -3 to 3, as said below
- summary_qkv_matrix: float32 [3, 64, 64], replicated, may hold values from -3 to 3
- exit_matrix: bfloat16 [512, 512], P('wid'), may hold values from -0.5 to 0.5
- widening_matrix: bfloat16 [512, 512], P('wid'), may hold values from -0.25 to 0.25
- narrowing_matrix: bfloat16 [512, 512], P('wid'), may hold values from -0.25 to 0.25
Outputs:
- result: bfloat16 [90112, 512], P(('pts', 'wid'))
Inputs may be any that keep to these rules, and one draw needn't show every extreme that they name: `vertex_features`: features of the points, of order one to ten. `entry_matrix`: weights of the point projection. `partition_matrix`: slice logit weights. `sharpness_matrix`: temperature weights.
All inputs are finite; a program needn't handle non-finite values.
Results may differ from a plain program's by a relative error of at most 0.013.
Values may be sent and summed in bfloat16 or wider, within the bound.
A program may use at most 128 MiB of HBM per device.

v0:
```python
import jax
import jax.numpy as jnp
from jax import lax
from jax.sharding import PartitionSpec as P


def layer_norm(values):
    centred = values - jnp.mean(values, axis=-1, keepdims=True)
    variance = jnp.mean(centred * centred, axis=-1, keepdims=True)
    return centred * lax.rsqrt(variance + 1e-05)


def project_tokens(token_rows, summary_qkv_matrix):
    highest = lax.Precision.HIGHEST
    queries = jnp.einsum("hgd,de->hge", token_rows, summary_qkv_matrix[0], precision=highest)
    keys_all = jnp.einsum("hgd,de->hge", token_rows, summary_qkv_matrix[1], precision=highest)
    value_rows_total = jnp.einsum(
        "hgd,de->hge", token_rows, summary_qkv_matrix[2], precision=highest
    )
    return (queries, keys_all, value_rows_total)


def local(
    vertex_features,
    entry_matrix,
    partition_matrix,
    sharpness_matrix,
    summary_qkv_matrix,
    exit_matrix,
    widening_matrix,
    narrowing_matrix,
):
    head_size = summary_qkv_matrix.shape[1]
    point_rows = vertex_features.shape[0]
    wid_count = lax.axis_size("wid")
    row_block = point_rows // wid_count
    features = vertex_features.astype(jnp.float32)
    normed = layer_norm(features).astype(jnp.bfloat16)
    feats = jnp.dot(normed, entry_matrix, preferred_element_type=jnp.float32).astype(jnp.bfloat16)
    local_heads = feats.shape[1] // head_size
    attention_cluster = feats.reshape(point_rows, local_heads, head_size)
    partition_sharpness = 0.5 + jax.nn.softplus(
        jnp.einsum(
            "kgv,v->kg", attention_cluster, sharpness_matrix, preferred_element_type=jnp.float32
        )
    )
    partition_scores = jnp.einsum(
        "nhd,dg->nhg", attention_cluster, partition_matrix, preferred_element_type=jnp.float32
    )
    partition_mapping = jax.nn.softmax(
        partition_scores / partition_sharpness[:, :, None], axis=-1
    ).astype(jnp.bfloat16)
    numerator = jnp.einsum(
        "nhg,nhd->hgd", partition_mapping, attention_cluster, preferred_element_type=jnp.float32
    )
    mass = jnp.sum(partition_mapping, axis=0, dtype=jnp.float32)
    numerator, mass = lax.psum((numerator, mass), "pts")
    token_rows = numerator / (mass[:, :, None] + 1e-05)
    queries, keys_all, value_rows_total = project_tokens(token_rows, summary_qkv_matrix)
    highest = lax.Precision.HIGHEST
    scores = jnp.einsum("hge,hke->hgk", queries, keys_all, precision=highest) / jnp.sqrt(
        jnp.float32(head_size)
    )
    attend = jax.nn.softmax(scores, axis=-1)
    out_tok = jnp.einsum("hgk,hke->hge", attend, value_rows_total, precision=highest).astype(
        jnp.bfloat16
    )
    deslice = jnp.einsum(
        "nhg,hgd->nhd", partition_mapping, out_tok, preferred_element_type=jnp.float32
    ).astype(jnp.bfloat16)
    deslice = deslice.reshape(point_rows, local_heads * head_size)
    mixed_rows = lax.all_to_all(deslice, "wid", split_axis=0, concat_axis=1, tiled=True)
    out_full, up_full, down_full = (
        lax.all_gather(exit_matrix, "wid", axis=0, tiled=True),
        lax.all_gather(widening_matrix, "wid", axis=0, tiled=True),
        lax.all_gather(narrowing_matrix, "wid", axis=0, tiled=True),
    )
    attn_rows = jnp.dot(mixed_rows, out_full, preferred_element_type=jnp.float32)
    own_rows = lax.dynamic_slice_in_dim(features, lax.axis_index("wid") * row_block, row_block, 0)
    midway = own_rows + attn_rows
    normed2 = layer_norm(midway).astype(jnp.bfloat16)
    hidden = jax.nn.gelu(jnp.dot(normed2, up_full, preferred_element_type=jnp.float32)).astype(
        jnp.bfloat16
    )
    return (midway + jnp.dot(hidden, down_full, preferred_element_type=jnp.float32)).astype(
        jnp.bfloat16
    )


def solution(mesh):
    placed = (
        P("pts", None),
        P(None, "wid"),
        P(),
        P(),
        P(),
        P("wid", None),
        P("wid", None),
        P("wid", None),
    )
    return jax.shard_map(
        local, mesh=mesh, in_specs=placed, out_specs=P(("pts", "wid"), None), check_vma=False
    )
```

profile of v0, /device:TPU:0, one launch (start us, length us, event | category | flops | bytes accessed | tf_op | source)
XLA Modules:
  0.0 224.7 jit_solution(1888954604760041601)
XLA Ops:
  0.0 0.0 copy-start
  0.0 14.9 %copy.12 = bf16[11264,512]{0,1:T(8,128)(2,1)} copy(bf16[11264,512]{1,0:T(8,128)(2,1)} %param.8) | data formatting | bytes 23068672 | tf_op args[0]
  14.9 7.2 %convert_reduce_fusion = f32[11264]{0:T(1024)S(1)} fusion(bf16[11264,512]{0,1:T(8,128)(2,1)} %copy.12), kind=kLoop, calls=%fused_computation.3 | loop fusion | flops 11523072 | bytes 11579392 | tf_op jit(solution)/shard_map/reduce_sum | solution.py:8
  22.0 7.4 %multiply_reduce_fusion = f32[11264]{0:T(1024)S(1)} fusion(bf16[11264,512]{0,1:T(8,128)(2,1)} %copy.12, f32[11264]{0:T(1024)S(1)} %broadcast_multiply_fusion), kind=kLoop, calls=%fused_computation.2 | loop fusion | flops 23057408 | bytes 11624448 | tf_op jit(solution)/shard_map/reduce_sum | solution.py:9
  29.5 0.0 copy-done
  29.5 0.0 copy-start.6
  29.5 8.1 %convolution_convert_fusion.1 = bf16[11264,128]{0,1:T(8,128)(2,1)S(1)} fusion(bf16[512,128]{1,0:T(8,128)(2,1)S(1)} %copy-done, bf16[11264,512]{0,1:T(8,128)(2,1)} %copy.12, f32[11264]{0:T(1024)S(1)} %add_rsqrt_fusion, f32[11264]{0:T(1024)S(1)} %broadcast_multiply_fusion), kind=kOutput, calls=%fused_computation.5 | convolution fusion | flops 1500905472 | bytes 14639104 | tf_op jit(solution)/shard_map/dot_general | solution.py:39
  37.6 0.0 copy-start.3
  37.6 0.0 copy-done.6
  37.6 5.4 %fusion.48 = f32[1,11264,2]{0,1,2:T(8,128)} fusion(bf16[11264,2,64]{0,2,1:T(8,128)(2,1)S(1)} %bitcast.68, f32[64]{0:T(128)S(1)} %copy-done.6), kind=kOutput, calls=%fused_computation.70 | convolution fusion | flops 2883584 | bytes 2973952 | tf_op jit(solution)/shard_map/kgv,v->kg/dot_general | solution.py:43
  43.0 0.0 copy-start.8
  43.0 6.6 %copy.16 = f32[1,11264,2]{1,2,0:T(2,128)S(1)} copy(f32[1,11264,2]{0,1,2:T(8,128)} %fusion.48) | data formatting | bytes 180224 | tf_op jit(solution)/shard_map/kgv,v->kg/dot_general | solution.py:43
  49.6 0.2 fusion.17
  49.8 0.0 copy-done.3
  49.8 0.0 copy-done.8
  49.8 2.9 %fusion.43 = (f32[11264,2]{0,1:T(2,128)S(1)}, f32[11264,2,32]{0,2,1:T(8,128)}) fusion(bf16[11264,2,64]{0,2,1:T(8,128)(2,1)S(1)} %bitcast.69, f32[11264,2]{0,1:T(2,128)S(1)} %fusion.17, bf16[64,32]{0,1:T(8,128)(2,1)S(1)} %copy-done.8), kind=kOutput, calls=%fused_computation.67 | convolution fusion | flops 94437408 | bytes 5951488 | tf_op jit(solution)/shard_map/sub | solution.py:50
  52.7 0.0 copy-start.7
  52.7 2.3 %convert_reduce_fusion.1 = (f32[2,32]{1,0:T(2,128)S(1)}, bf16[11264,2,32]{0,2,1:T(8,128)(2,1)S(1)}) fusion(f32[11264,2,32]{0,2,1:T(8,128)} %get-tuple-element.10, f32[11264,2]{0,1:T(2,128)S(1)} %get-tuple-element.9), kind=kLoop, calls=%fused_computation.28 | loop fusion | flops 2883520 | bytes 4415744 | tf_op jit(solution)/shard_map/reduce_sum | solution.py:56
  55.1 2.7 %fusion.51 = f32[2,32,64]{2,1,0:T(8,128)S(1)} fusion(bf16[11264,2,32]{0,2,1:T(8,128)(2,1)S(1)} %get-tuple-element.8, bf16[11264,2,64]{0,2,1:T(8,128)(2,1)} %bitcast.70), kind=kOutput, calls=%fused_computation.72 | convolution fusion | flops 92274688 | bytes 4341760 | tf_op jit(solution)/shard_map/nhg,nhd->hgd/dot_general | solution.py:53
  57.7 25.9 %all-reduce = (f32[2,32,64]{2,1,0:T(8,128)S(1)}, f32[2,32]{1,0:T(2,128)S(1)}) all-reduce(f32[2,32,64]{2,1,0:T(8,128)S(1)} %fusion.51, f32[2,32]{1,0:T(2,128)S(1)} %get-tuple-element.7), channel_id=1, replica_groups=mesh['pts'=8,'wid'=4] {'pts'}, use_global_device_ids=true, to_apply=%region_4.5 | all-reduce | flops 4160 | bytes 33280 | tf_op jit(solution)/shard_map/psum | solution.py:57
  83.6 0.0 copy-done.7
  83.6 0.2 fusion.24
  83.8 0.2 fusion.26
  84.1 0.2 fusion.22
  84.3 0.2 fusion.44
  84.6 0.3 convolution_convert_fusion.2
  84.8 2.5 %fusion.2 = bf16[11264,2,64]{0,2,1:T(8,128)(2,1)} fusion(bf16[2,32,64]{2,1,0:T(8,128)(2,1)S(1)} %convolution_convert_fusion.2, bf16[11264,2,32]{0,2,1:T(8,128)(2,1)S(1)} %get-tuple-element.8), kind=kOutput, calls=%fused_computation.7 | convolution fusion | flops 93716480 | bytes 4333568 | tf_op jit(solution)/shard_map/nhg,hgd->nhd/dot_general | solution.py:68
  87.3 5.3 %all_to_all.14 = bf16[4,2816,128]{1,0,2:T(4,128)(2,1)S(1)} reshape(bf16[11264,2,64]{0,2,1:T(8,128)(2,1)} %fusion.2) | data formatting | bytes 5767168 | tf_op jit(solution)/shard_map/all_to_all | solution.py:72
  92.6 1.9 copy.13
  94.5 4.9 %all-to-all-start = ((bf16[4,2816,128]{1,2,0:T(8,128)(2,1)}), bf16[4,2816,128]{1,2,0:T(8,128)(2,1)S(1)}, u32[]{:S(2)}, u32[]{:S(2)}) async-start(bf16[4,2816,128]{1,2,0:T(8,128)(2,1)} %copy.13), calls=%async_computation | async-start | bytes 5767168 | tf_op jit(solution)/shard_map/all_to_all | solution.py:72
  99.4 0.0 copy-start.5
  99.4 13.0 %convert_element_type.33 = f32[11264,512]{0,1:T(8,128)} convert(bf16[11264,512]{0,1:T(8,128)(2,1)} %copy.12) | non-fusion elementwise | flops 5767168 | bytes 34603008 | tf_op jit(solution)/shard_map/convert_element_type | solution.py:37
  112.3 0.0 copy-done.5
  112.3 60.0 %all_gather.9 = bf16[512,512]{1,0:T(8,128)(2,1)S(1)} all-gather(bf16[128,512]{1,0:T(8,128)(2,1)S(1)} %copy-done.5), channel_id=1, replica_groups=mesh['pts'=8,'wid'=4] {'wid'}, dimensions={0}, use_global_device_ids=true | all-gather | bytes 655360 | tf_op jit(solution)/shard_map/all_gather | solution.py:74
  172.3 17.7 %all_gather.10 = bf16[512,512]{1,0:T(8,128)(2,1)} all-gather(bf16[128,512]{1,0:T(8,128)(2,1)} %param.14), channel_id=1, replica_groups=mesh['pts'=8,'wid'=4] {'wid'}, dimensions={0}, use_global_device_ids=true | all-gather | bytes 655360 | tf_op jit(solution)/shard_map/all_gather | solution.py:75
  190.1 16.3 %all_gather.11 = bf16[512,512]{1,0:T(8,128)(2,1)} all-gather(bf16[128,512]{1,0:T(8,128)(2,1)} %param.15), channel_id=1, replica_groups=mesh['pts'=8,'wid'=4] {'wid'}, dimensions={0}, use_global_device_ids=true | all-gather | bytes 655360 | tf_op jit(solution)/shard_map/all_gather | solution.py:76
  206.3 0.0 all-to-all-done
  206.3 4.4 %fusion.45 = (f32[2816]{0:T(1024)S(1)}, f32[2816,512]{0,1:T(8,128)S(1)}) fusion(bf16[2816,512]{0,1:T(8,128)(2,1)S(1)} %bitcast.67, bf16[512,512]{1,0:T(8,128)(2,1)S(1)} %all_gather.9, f32[11264,512]{0,1:T(8,128)} %convert_element_type.33, s32[]{:T(128)S(6)} %select_n.7), kind=kOutput, calls=%fused_computation.69 | convolution fusion | flops 1479275776 | bytes 14953476 | tf_op jit(solution)/shard_map/dot_general | solution.py:78
  210.7 0.0 copy-start.2
  210.7 0.0 copy-start.4
  210.7 2.4 %copy-done.2 = f32[2816,512]{0,1:T(8,128)} copy-done((f32[2816,512]{0,1:T(8,128)}, f32[2816,512]{0,1:T(8,128)S(1)}, u32[]{:S(2)}) %copy-start.2) | copy-done | bytes 5767192
  213.2 0.6 multiply_reduce_fusion.1
  213.8 0.6 add_rsqrt_fusion.1
  214.4 0.0 copy-done.4
  214.4 0.0 copy-start.1
  214.4 7.6 %add_convert_fusion = bf16[2816,512]{0,1:T(8,128)(2,1)S(1)} fusion(f32[2816,512]{0,1:T(8,128)} %copy-done.2, bf16[512,512]{1,0:T(8,128)(2,1)} %all_gather.11, bf16[512,512]{1,0:T(8,128)(2,1)S(1)} %copy-done.4, f32[2816]{0:T(1024)} %add_rsqrt_fusion.1, f32[2816]{0:T(1024)S(1)} %broadcast_multiply_fusion.1), kind=kOutput, calls=%fused_computation.21 | convolution fusion | flops 2972975104 | bytes 9721856 | tf_op jit(solution)/shard_map/dot_general | solution.py:85
  222.0 2.7 %copy.15 = bf16[2816,512]{1,0:T(8,128)(2,1)} copy(bf16[2816,512]{0,1:T(8,128)(2,1)S(1)} %add_convert_fusion) | data formatting | bytes 5767168 | tf_op jit(solution)/shard_map/convert_element_type | solution.py:85
  224.7 0.0 copy-done.1
  (5 shorter events, 0.1 us)
Async XLA Ops:
  0.0 29.5 %copy-start = (bf16[512,128]{1,0:T(8,128)(2,1)S(1)}, bf16[512,128]{1,0:T(8,128)(2,1)}, u32[]{:S(2)}) copy-start(bf16[512,128]{1,0:T(8,128)(2,1)} %param.9) | copy-start | bytes 393220
  29.5 8.1 %copy-start.6 = (f32[64]{0:T(128)S(1)}, f32[64]{0:T(128)}, u32[]{:S(2)}) copy-start(f32[64]{0:T(128)} %param.11) | copy-start | bytes 772
  37.6 12.2 %copy-start.3 = (bf16[11264,128]{0,1:T(8,128)(2,1)}, bf16[11264,128]{0,1:T(8,128)(2,1)S(1)}, u32[]{:S(2)}) copy-start(bf16[11264,128]{0,1:T(8,128)(2,1)S(1)} %convolution_convert_fusion.1) | copy-start | bytes 8650756
  43.0 6.8 %copy-start.8 = (bf16[64,32]{0,1:T(8,128)(2,1)S(1)}, bf16[64,32]{0,1:T(8,128)(2,1)}, u32[]{:S(2)}) copy-start(bf16[64,32]{0,1:T(8,128)(2,1)} %param.10) | copy-start | bytes 12292
  52.7 30.9 %copy-start.7 = (f32[3,64,64]{2,1,0:T(8,128)S(1)}, f32[3,64,64]{2,1,0:T(8,128)}, u32[]{:S(2)}) copy-start(f32[3,64,64]{2,1,0:T(8,128)} %param.12) | copy-start | bytes 147460
  94.5 111.9 %all-to-all-start = ((bf16[4,2816,128]{1,2,0:T(8,128)(2,1)}), bf16[4,2816,128]{1,2,0:T(8,128)(2,1)S(1)}, u32[]{:S(2)}, u32[]{:S(2)}) async-start(bf16[4,2816,128]{1,2,0:T(8,128)(2,1)} %copy.13), calls=%async_computation | async-start | bytes 5767168 | tf_op jit(solution)/shard_map/all_to_all | solution.py:72
  99.4 13.0 %copy-start.5 = (bf16[128,512]{1,0:T(8,128)(2,1)S(1)}, bf16[128,512]{1,0:T(8,128)(2,1)}, u32[]{:S(2)}) copy-start(bf16[128,512]{1,0:T(8,128)(2,1)} %param.13) | copy-start | bytes 393220
  210.7 2.5 %copy-start.2 = (f32[2816,512]{0,1:T(8,128)}, f32[2816,512]{0,1:T(8,128)S(1)}, u32[]{:S(2)}) copy-start(f32[2816,512]{0,1:T(8,128)S(1)} %get-tuple-element.14) | copy-start | bytes 17301508
  210.7 3.7 %copy-start.4 = (bf16[512,512]{1,0:T(8,128)(2,1)S(1)}, bf16[512,512]{1,0:T(8,128)(2,1)}, u32[]{:S(2)}) copy-start(bf16[512,512]{1,0:T(8,128)(2,1)} %all_gather.10) | copy-start | bytes 1572868
  214.4 10.3 %copy-start.1 = (bf16[512,128]{1,0:T(8,128)(2,1)S(1)}, bf16[512,128]{1,0:T(8,128)(2,1)}, u32[]{:S(2)}) copy-start(bf16[512,128]{1,0:T(8,128)(2,1)} %param.9) | copy-start | bytes 393220
where the time goes:
time: 226 us; the launch traced here: 225 us
  blocking collectives  120 us (53%)
  matrix products  34.7 us (15%)
  local copies, waits for them, and re-layouts  33.8 us (15%)
  other arithmetic  31.3 us (14%)
  starting transfers between devices  4.87 us (2%)
    all_gather x1, blocking collectives, local(): lax.all_gather(exit_matrix, 'wid', axis=0, tiled=True)  60 us
    psum x1, blocking collectives, local(): numerator, mass = lax.psum((numerator, mass), 'pts')  25.9 us
    all_gather x1, blocking collectives, local(): lax.all_gather(widening_matrix, 'wid', axis=0, tiled=True)  17.7 us
    unnamed x19, local copies, waits for them, and re-layouts  17.3 us
    all_gather x1, blocking collectives, local(): lax.all_gather(narrowing_matrix, 'wid', axis=0, tiled=True)  16.3 us
    convert_element_type x1, other arithmetic, local(): features = vertex_features.astype(jnp.float32)  13 us
    dot_general x1, matrix products, local(): jnp.dot(normed, entry_matrix, preferred_element_type=jnp.float32)  8.08 us
    reduce_sum x2, other arithmetic, layer_norm(): variance = jnp.mean(centred * centred, axis=-1, keepdims=True)  8.01 us
  transfers between devices with their start and end apart: 1, of which 0 were waited for; matrix products, arithmetic and copies ran while one was open for 6% of the time, Pallas kernels for 0%

commit v1 on v0

--- a/solution.py
+++ b/solution.py
@@ -69,7 +69,10 @@
         "nhg,hgd->nhd", partition_mapping, out_tok, preferred_element_type=jnp.float32
     ).astype(jnp.bfloat16)
     deslice = deslice.reshape(point_rows, local_heads * head_size)
-    mixed_rows = lax.all_to_all(deslice, "wid", split_axis=0, concat_axis=1, tiled=True)
+    mixed_rows = jnp.concatenate(
+        lax.all_to_all(jnp.stack(jnp.split(deslice, lax.axis_size("wid"), axis=0)), "wid", 0, 0),
+        axis=1,
+    )
     out_full, up_full, down_full = (
         lax.all_gather(exit_matrix, "wid", axis=0, tiled=True),
         lax.all_gather(widening_matrix, "wid", axis=0, tiled=True),

time: 226 us -> 219 us (0.969)
  local copies, waits for them, and re-layouts: 33.8 us -> 26.9 us
    all_to_all x2 -> x0, local copies, waits for them, and re-layouts: 7.14 us -> none  [local(): lax.all_to_all(deslice, 'wid', split_axis=0, concat_axis=1, tiled=True)]
where the time goes in v1:
time: 219 us; the launch traced here: 218 us
  blocking collectives  120 us (55%)
  other arithmetic  33.1 us (15%)
  matrix products  33.1 us (15%)
  local copies, waits for them, and re-layouts  26.9 us (12%)
  starting transfers between devices  4.87 us (2%)
    all_gather x1, blocking collectives, local(): lax.all_gather(exit_matrix, 'wid', axis=0, tiled=True)  60 us
    psum x1, blocking collectives, local(): numerator, mass = lax.psum((numerator, mass), 'pts')  25.9 us
    all_gather x1, blocking collectives, local(): lax.all_gather(widening_matrix, 'wid', axis=0, tiled=True)  17.7 us
    unnamed x19, local copies, waits for them, and re-layouts  17.3 us
    all_gather x1, blocking collectives, local(): lax.all_gather(narrowing_matrix, 'wid', axis=0, tiled=True)  16.3 us
    convert_element_type x1, other arithmetic, local(): features = vertex_features.astype(jnp.float32)  13 us
    dot_general x1, matrix products, local(): jnp.dot(normed, entry_matrix, preferred_element_type=jnp.float32)  8.08 us
    reduce_sum x2, other arithmetic, layer_norm(): variance = jnp.mean(centred * centred, axis=-1, keepdims=True)  8.01 us
  transfers between devices with their start and end apart: 1, of which 0 were waited for; matrix products, arithmetic and copies ran while one was open for 6% of the time, Pallas kernels for 0%

profile of v1, /device:TPU:0, one launch (start us, length us, event | category | flops | bytes accessed | tf_op | source)
XLA Modules:
  0.0 218.0 jit_solution(1795988380376830576)
XLA Ops:
  0.0 0.0 copy-start
  0.0 14.9 %copy.9 = bf16[11264,512]{0,1:T(8,128)(2,1)} copy(bf16[11264,512]{1,0:T(8,128)(2,1)} %param.8) | data formatting | bytes 23068672 | tf_op args[0]
  14.9 7.2 %convert_reduce_fusion = f32[11264]{0:T(1024)S(1)} fusion(bf16[11264,512]{0,1:T(8,128)(2,1)} %copy.9), kind=kLoop, calls=%fused_computation.3 | loop fusion | flops 11523072 | bytes 11579392 | tf_op jit(solution)/shard_map/reduce_sum | solution.py:8
  22.0 7.4 %multiply_reduce_fusion = f32[11264]{0:T(1024)S(1)} fusion(bf16[11264,512]{0,1:T(8,128)(2,1)} %copy.9, f32[11264]{0:T(1024)S(1)} %broadcast_multiply_fusion), kind=kLoop, calls=%fused_computation.2 | loop fusion | flops 23057408 | bytes 11624448 | tf_op jit(solution)/shard_map/reduce_sum | solution.py:9
  29.5 0.0 copy-done
  29.5 0.0 copy-start.6
  29.5 8.1 %convolution_convert_fusion.1 = bf16[11264,128]{0,1:T(8,128)(2,1)S(1)} fusion(bf16[512,128]{1,0:T(8,128)(2,1)S(1)} %copy-done, bf16[11264,512]{0,1:T(8,128)(2,1)} %copy.9, f32[11264]{0:T(1024)S(1)} %add_rsqrt_fusion, f32[11264]{0:T(1024)S(1)} %broadcast_multiply_fusion), kind=kOutput, calls=%fused_computation.5 | convolution fusion | flops 1500905472 | bytes 14639104 | tf_op jit(solution)/shard_map/dot_general | solution.py:39
  37.6 0.0 copy-start.3
  37.6 0.0 copy-done.6
  37.6 5.4 %fusion.49 = f32[1,11264,2]{0,1,2:T(8,128)} fusion(bf16[11264,2,64]{0,2,1:T(8,128)(2,1)S(1)} %bitcast.70, f32[64]{0:T(128)S(1)} %copy-done.6), kind=kOutput, calls=%fused_computation.72 | convolution fusion | flops 2883584 | bytes 2973952 | tf_op jit(solution)/shard_map/kgv,v->kg/dot_general | solution.py:43
  43.0 0.0 copy-start.8
  43.0 6.6 %copy.12 = f32[1,11264,2]{1,2,0:T(2,128)S(1)} copy(f32[1,11264,2]{0,1,2:T(8,128)} %fusion.49) | data formatting | bytes 180224 | tf_op jit(solution)/shard_map/kgv,v->kg/dot_general | solution.py:43
  49.6 0.2 fusion.17
  49.8 0.0 copy-done.3
  49.8 0.0 copy-done.8
  49.8 2.9 %fusion.44 = (f32[11264,2]{0,1:T(2,128)S(1)}, f32[11264,2,32]{0,2,1:T(8,128)}) fusion(bf16[11264,2,64]{0,2,1:T(8,128)(2,1)S(1)} %bitcast.71, f32[11264,2]{0,1:T(2,128)S(1)} %fusion.17, bf16[64,32]{0,1:T(8,128)(2,1)S(1)} %copy-done.8), kind=kOutput, calls=%fused_computation.69 | convolution fusion | flops 94437408 | bytes 5951488 | tf_op jit(solution)/shard_map/sub | solution.py:50
  52.7 0.0 copy-start.7
  52.7 2.3 %convert_reduce_fusion.1 = (f32[2,32]{1,0:T(2,128)S(1)}, bf16[11264,2,32]{0,2,1:T(8,128)(2,1)S(1)}) fusion(f32[11264,2,32]{0,2,1:T(8,128)} %get-tuple-element.14, f32[11264,2]{0,1:T(2,128)S(1)} %get-tuple-element.13), kind=kLoop, calls=%fused_computation.29 | loop fusion | flops 2883520 | bytes 4415744 | tf_op jit(solution)/shard_map/reduce_sum | solution.py:56
  55.1 2.7 %fusion.52 = f32[2,32,64]{2,1,0:T(8,128)S(1)} fusion(bf16[11264,2,32]{0,2,1:T(8,128)(2,1)S(1)} %get-tuple-element.8, bf16[11264,2,64]{0,2,1:T(8,128)(2,1)} %bitcast.72), kind=kOutput, calls=%fused_computation.74 | convolution fusion | flops 92274688 | bytes 4341760 | tf_op jit(solution)/shard_map/nhg,nhd->hgd/dot_general | solution.py:53
  57.7 25.9 %all-reduce = (f32[2,32,64]{2,1,0:T(8,128)S(1)}, f32[2,32]{1,0:T(2,128)S(1)}) all-reduce(f32[2,32,64]{2,1,0:T(8,128)S(1)} %fusion.52, f32[2,32]{1,0:T(2,128)S(1)} %get-tuple-element.7), channel_id=1, replica_groups=mesh['pts'=8,'wid'=4] {'pts'}, use_global_device_ids=true, to_apply=%region_4.5 | all-reduce | flops 4160 | bytes 33280 | tf_op jit(solution)/shard_map/psum | solution.py:57
  83.6 0.0 copy-done.7
  83.6 0.2 fusion.24
  83.8 0.2 fusion.26
  84.1 0.2 fusion.22
  84.3 0.2 fusion.45
  84.6 0.3 convolution_convert_fusion.2
  84.8 0.9 fusion.2
  85.8 0.2 fusion.43
  86.0 1.8 pad_maximum_fusion
  87.8 4.9 %all-to-all-start = ((bf16[4,2816,128]{1,2,0:T(8,128)(2,1)}), bf16[4,2816,128]{1,2,0:T(8,128)(2,1)S(1)}, u32[]{:S(2)}, u32[]{:S(2)}) async-start(bf16[4,2816,128]{1,2,0:T(8,128)(2,1)} %pad_maximum_fusion), calls=%async_computation | async-start | bytes 5767168 | tf_op jit(solution)/shard_map/all_to_all | solution.py:73
  92.6 0.0 copy-start.5
  92.6 13.0 %convert_element_type.33 = f32[11264,512]{0,1:T(8,128)} convert(bf16[11264,512]{0,1:T(8,128)(2,1)} %copy.9) | non-fusion elementwise | flops 5767168 | bytes 34603008 | tf_op jit(solution)/shard_map/convert_element_type | solution.py:37
  105.6 0.0 copy-done.5
  105.6 60.0 %all_gather.9 = bf16[512,512]{1,0:T(8,128)(2,1)S(1)} all-gather(bf16[128,512]{1,0:T(8,128)(2,1)S(1)} %copy-done.5), channel_id=1, replica_groups=mesh['pts'=8,'wid'=4] {'wid'}, dimensions={0}, use_global_device_ids=true | all-gather | bytes 655360 | tf_op jit(solution)/shard_map/all_gather | solution.py:77
  165.6 17.7 %all_gather.10 = bf16[512,512]{1,0:T(8,128)(2,1)} all-gather(bf16[128,512]{1,0:T(8,128)(2,1)} %param.14), channel_id=1, replica_groups=mesh['pts'=8,'wid'=4] {'wid'}, dimensions={0}, use_global_device_ids=true | all-gather | bytes 655360 | tf_op jit(solution)/shard_map/all_gather | solution.py:78
  183.3 16.3 %all_gather.11 = bf16[512,512]{1,0:T(8,128)(2,1)} all-gather(bf16[128,512]{1,0:T(8,128)(2,1)} %param.15), channel_id=1, replica_groups=mesh['pts'=8,'wid'=4] {'wid'}, dimensions={0}, use_global_device_ids=true | all-gather | bytes 655360 | tf_op jit(solution)/shard_map/all_gather | solution.py:79
  199.6 0.0 all-to-all-done
  199.6 4.4 %fusion.46 = (f32[2816]{0:T(1024)S(1)}, f32[2816,512]{0,1:T(8,128)S(1)}) fusion(bf16[2816,512]{0,1:T(8,128)(2,1)S(1)} %bitcast.69, bf16[512,512]{1,0:T(8,128)(2,1)S(1)} %all_gather.9, f32[11264,512]{0,1:T(8,128)} %convert_element_type.33, s32[]{:T(128)S(6)} %select_n.7), kind=kOutput, calls=%fused_computation.71 | convolution fusion | flops 1479275776 | bytes 14953476 | tf_op jit(solution)/shard_map/dot_general | solution.py:81
  204.0 0.0 copy-start.2
  204.0 0.0 copy-start.4
  204.0 2.4 %copy-done.2 = f32[2816,512]{0,1:T(8,128)} copy-done((f32[2816,512]{0,1:T(8,128)}, f32[2816,512]{0,1:T(8,128)S(1)}, u32[]{:S(2)}) %copy-start.2) | copy-done | bytes 5767192
  206.5 0.6 multiply_reduce_fusion.1
  207.1 0.6 add_rsqrt_fusion.1
  207.7 0.0 copy-done.4
  207.7 0.0 copy-start.1
  207.7 7.6 %add_convert_fusion = bf16[2816,512]{0,1:T(8,128)(2,1)S(1)} fusion(f32[2816,512]{0,1:T(8,128)} %copy-done.2, bf16[512,512]{1,0:T(8,128)(2,1)} %all_gather.11, bf16[512,512]{1,0:T(8,128)(2,1)S(1)} %copy-done.4, f32[2816]{0:T(1024)} %add_rsqrt_fusion.1, f32[2816]{0:T(1024)S(1)} %broadcast_multiply_fusion.1), kind=kOutput, calls=%fused_computation.21 | convolution fusion | flops 2972975104 | bytes 9721856 | tf_op jit(solution)/shard_map/dot_general | solution.py:88
  215.3 2.7 %copy.11 = bf16[2816,512]{1,0:T(8,128)(2,1)} copy(bf16[2816,512]{0,1:T(8,128)(2,1)S(1)} %add_convert_fusion) | data formatting | bytes 5767168 | tf_op jit(solution)/shard_map/convert_element_type | solution.py:88
  218.0 0.0 copy-done.1
  (5 shorter events, 0.1 us)
Async XLA Ops:
  0.0 29.5 %copy-start = (bf16[512,128]{1,0:T(8,128)(2,1)S(1)}, bf16[512,128]{1,0:T(8,128)(2,1)}, u32[]{:S(2)}) copy-start(bf16[512,128]{1,0:T(8,128)(2,1)} %param.9) | copy-start | bytes 393220
  29.5 8.1 %copy-start.6 = (f32[64]{0:T(128)S(1)}, f32[64]{0:T(128)}, u32[]{:S(2)}) copy-start(f32[64]{0:T(128)} %param.11) | copy-start | bytes 772
  37.6 12.2 %copy-start.3 = (bf16[11264,128]{0,1:T(8,128)(2,1)}, bf16[11264,128]{0,1:T(8,128)(2,1)S(1)}, u32[]{:S(2)}) copy-start(bf16[11264,128]{0,1:T(8,128)(2,1)S(1)} %convolution_convert_fusion.1) | copy-start | bytes 8650756
  43.0 6.8 %copy-start.8 = (bf16[64,32]{0,1:T(8,128)(2,1)S(1)}, bf16[64,32]{0,1:T(8,128)(2,1)}, u32[]{:S(2)}) copy-start(bf16[64,32]{0,1:T(8,128)(2,1)} %param.10) | copy-start | bytes 12292
  52.7 30.9 %copy-start.7 = (f32[3,64,64]{2,1,0:T(8,128)S(1)}, f32[3,64,64]{2,1,0:T(8,128)}, u32[]{:S(2)}) copy-start(f32[3,64,64]{2,1,0:T(8,128)} %param.12) | copy-start | bytes 147460
  87.8 111.9 %all-to-all-start = ((bf16[4,2816,128]{1,2,0:T(8,128)(2,1)}), bf16[4,2816,128]{1,2,0:T(8,128)(2,1)S(1)}, u32[]{:S(2)}, u32[]{:S(2)}) async-start(bf16[4,2816,128]{1,2,0:T(8,128)(2,1)} %pad_maximum_fusion), calls=%async_computation | async-start | bytes 5767168 | tf_op jit(solution)/shard_map/all_to_all | solution.py:73
  92.6 13.0 %copy-start.5 = (bf16[128,512]{1,0:T(8,128)(2,1)S(1)}, bf16[128,512]{1,0:T(8,128)(2,1)}, u32[]{:S(2)}) copy-start(bf16[128,512]{1,0:T(8,128)(2,1)} %param.13) | copy-start | bytes 393220
  204.0 2.5 %copy-start.2 = (f32[2816,512]{0,1:T(8,128)}, f32[2816,512]{0,1:T(8,128)S(1)}, u32[]{:S(2)}) copy-start(f32[2816,512]{0,1:T(8,128)S(1)} %get-tuple-element.18) | copy-start | bytes 17301508
  204.0 3.7 %copy-start.4 = (bf16[512,512]{1,0:T(8,128)(2,1)S(1)}, bf16[512,512]{1,0:T(8,128)(2,1)}, u32[]{:S(2)}) copy-start(bf16[512,512]{1,0:T(8,128)(2,1)} %all_gather.10) | copy-start | bytes 1572868
  207.7 10.3 %copy-start.1 = (bf16[512,128]{1,0:T(8,128)(2,1)S(1)}, bf16[512,128]{1,0:T(8,128)(2,1)}, u32[]{:S(2)}) copy-start(bf16[512,128]{1,0:T(8,128)(2,1)} %param.9) | copy-start | bytes 393220
